TPU v7x, 32 devices: a whole 2x2x4 slice. The times are simulated.
32 devices in a mesh: group: 2 (over y), ctx: 4 (over z), head: 2 (over x), req: 2 (over core).
Axes of the slice: x: 2, y: 2, z: 4, core: 2. Of those that a mesh axis runs over, the one named last changes fastest.
Arguments:
- fresh_hidden: bfloat16 [4, 512, 8192], P(('group', 'req'), 'ctx', 'head'), parts along dimension 0, may hold values from -6 to 6
- latent_down: bfloat16 [8192, 512], P('head'), may hold values from -0.0625 to 0.0625
- cache_latents: bfloat16 [4, 1024, 512], P(('group', 'req'), 'ctx', 'head'), parts along dimension 0, may hold values from -6 to 6
- key_up: bfloat16 [2, 256, 128], P('head'), may hold values from -0.375 to 0.375
- value_up: bfloat16 [2, 256, 128], P('head'), may hold values from -0.375 to 0.375
- queries: bfloat16 [4, 512, 2048], P(('group', 'req'), 'ctx', 'head'), parts along dimension 0, may hold values from -160 to 160
- span_start: int32 [4, 4], P(('group', 'req')), parts along dimension 0, may hold values from 0 to 3, as said below
Outputs:
- attention: bfloat16 [4, 512, 2048], P(('group', 'req'), 'ctx', 'head'), parts along dimension 0
There are 2 independent parts, one for each index of `group`. A program takes and returns all parts, laid end to end along the dimension named above; an argument that names none is the same for every part. Nothing has to cross between parts.
Inputs may be any that keep to these rules, and one draw needn't show every extreme that they name: For each request span_start is a permutation of 0 to 4 - 1 over the spans.
All inputs are finite; a program needn't handle non-finite values.
Results may differ from a plain program's by a relative error of at most 0.035.
Values may be sent and summed in bfloat16 or wider, within the bound.
No kernel may reach another device: no remote copies, remote signals or barrier semaphores. Data moves between devices by JAX's collectives and lax.ppermute only.
A program may use at most 128 MiB of HBM per device.

v0:
```python
import jax
import jax.numpy as jnp
from jax import lax
from jax.sharding import PartitionSpec as P

ROPE_BASE = 500000.0
SCORE_FLOOR = -1e30


def rotate(field, positions):
    half_dim = field.shape[-1] // 2
    inv_freq = ROPE_BASE ** (-(jnp.arange(half_dim, dtype=jnp.float32) * 2.0 / field.shape[-1]))
    angles = positions.astype(jnp.float32)[:, None] * inv_freq[None, :]
    cosine = jnp.cos(angles)
    sine_part = jnp.sin(angles)
    first_half = field[..., :half_dim]
    second_half = field[..., half_dim:]
    return jnp.concatenate(
        [
            first_half * cosine - second_half * sine_part,
            second_half * cosine + first_half * sine_part,
        ],
        axis=-1,
    )


def rebuild(latents, positions, key_up, value_up, rank_width):
    key_rows = rotate(
        jnp.dot(latents[:, :rank_width], key_up[0], preferred_element_type=jnp.float32), positions
    ).astype(jnp.bfloat16)
    value_rows = jnp.dot(
        latents[:, rank_width:], value_up[0], preferred_element_type=jnp.float32
    ).astype(jnp.bfloat16)
    return (key_rows, value_rows)


def attend(state_in, query_rows, row_pos, key_rows, value_rows, positions, score_scale):
    row_max, row_sum, weighted = state_in
    scores = (
        lax.dot_general(
            query_rows, key_rows, (((1,), (1,)), ((), ())), preferred_element_type=jnp.float32
        )
        * score_scale
    )
    visible = positions[None, :] <= row_pos[:, None]
    scores = jnp.where(visible, scores, SCORE_FLOOR)
    new_max = jnp.maximum(row_max, jnp.max(scores, axis=1))
    weights = jnp.where(visible, jnp.exp(scores - new_max[:, None]), 0.0)
    row_sum = jnp.sum(weights, axis=1)
    weighted = jnp.dot(weights.astype(jnp.bfloat16), value_rows, preferred_element_type=jnp.float32)
    return (new_max, row_sum, weighted)


def guarded(state_in, query_rows, row_pos, key_rows, value_rows, positions, score_scale):
    return attend(state_in, query_rows, row_pos, key_rows, value_rows, positions, score_scale)


def per_device(fresh_hidden, latent_down, cache_latents, key_up, value_up, queries, span_start):
    partial_value = jnp.dot(fresh_hidden[0], latent_down, preferred_element_type=jnp.float32)
    fresh_lat = lax.psum(partial_value, "head").astype(jnp.bfloat16)
    cache_full = lax.all_gather(cache_latents, "head", axis=2, tiled=True)[0]
    local_lat = jnp.concatenate([cache_full, fresh_lat], axis=0)
    tok_dev = local_lat.shape[0]
    rank_width = local_lat.shape[1] // 2
    fresh_dev = queries.shape[1]
    cache_dev = tok_dev - fresh_dev
    head_dim = key_up.shape[2]
    per_kv = queries.shape[2] // head_dim
    score_scale = head_dim ** (-0.5)
    places = span_start[0]
    span_count = places.shape[0]
    cache_total = cache_dev * span_count
    span_id = lax.axis_index("ctx")
    own_place = lax.dynamic_index_in_dim(places, span_id, keepdims=False)
    query_pos = cache_total + own_place * fresh_dev + jnp.arange(fresh_dev, dtype=jnp.int32)
    cache_pos = places[:, None] * cache_dev + jnp.arange(cache_dev, dtype=jnp.int32)[None, :]
    fresh_pos = (
        cache_total + places[:, None] * fresh_dev + jnp.arange(fresh_dev, dtype=jnp.int32)[None, :]
    )
    key_pos_all = jnp.concatenate([cache_pos, fresh_pos], axis=1).reshape(-1)
    query_heads = (
        queries[0].reshape(fresh_dev, per_kv, head_dim).transpose(1, 0, 2).astype(jnp.float32)
    )
    query_rows = (
        rotate(query_heads, query_pos).astype(jnp.bfloat16).reshape(per_kv * fresh_dev, head_dim)
    )
    row_pos = jnp.tile(query_pos, per_kv)
    row_count = per_kv * fresh_dev
    initial = (
        jnp.full((row_count,), SCORE_FLOOR, jnp.float32),
        jnp.zeros((row_count,), jnp.float32),
        jnp.zeros((row_count, head_dim), jnp.float32),
    )
    own_pos = lax.dynamic_slice_in_dim(key_pos_all, span_id * tok_dev, tok_dev)
    own_keys, own_values = rebuild(local_lat, own_pos, key_up, value_up, rank_width)
    state = guarded(
        initial,
        query_rows,
        row_pos,
        lax.all_gather(own_keys, "ctx", axis=0, tiled=True),
        lax.all_gather(own_values, "ctx", axis=0, tiled=True),
        key_pos_all,
        score_scale,
    )
    row_max, row_sum, weighted = state
    mixed = (weighted / row_sum[:, None]).astype(jnp.bfloat16)
    mixed = (
        mixed.reshape(per_kv, fresh_dev, head_dim)
        .transpose(1, 0, 2)
        .reshape(1, fresh_dev, per_kv * head_dim)
    )
    return mixed


def solution(mesh):
    return jax.shard_map(
        per_device,
        mesh=mesh,
        in_specs=(
            P(("group", "req"), "ctx", "head"),
            P("head", None),
            P(("group", "req"), "ctx", "head"),
            P("head", None, None),
            P("head", None, None),
            P(("group", "req"), "ctx", "head"),
            P(("group", "req"), None),
        ),
        out_specs=P(("group", "req"), "ctx", "head"),
        check_vma=False,
    )
```

profile of v0, /device:TPU:0, one launch (start us, length us, event | category | flops | bytes accessed | tf_op | source)
XLA Modules:
  0.0 63.9 jit_solution(10641969654796852829)
XLA Ops:
  0.0 0.0 copy-start
  0.0 0.0 copy-start.1
  0.0 0.0 copy-start.2
  0.0 0.0 copy-start.3
  0.0 1.3 %fusion.38 = s32[1,1]{1,0:T(1,128)} fusion(s32[1,4]{1,0:T(1,128)} %param.13, s32[]{:T(128)S(6)} %select_n.14), kind=kLoop, calls=%fused_computation.59 | loop fusion | flops 1 | bytes 12 | tf_op jit(solution)/shard_map/mul | solution.py:75
  2.1 0.7 %multiply_bitcast_fusion = (s32[4]{0:T(128)S(1)}, s32[4]{0:T(128)S(1)}) fusion(s32[1,4]{1,0:T(1,128)} %param.13), kind=kLoop, calls=%fused_computation.50 | loop fusion | flops 12 | bytes 48 | tf_op jit(solution)/shard_map/mul | solution.py:76
  2.7 0.1 iota_add_fusion.1
  2.8 0.1 iota_add_fusion
  2.9 0.1 dynamic-slice_convert_fusion
  3.0 0.2 multiply_cosine_fusion.1
  3.2 0.0 copy-done
  3.2 2.9 %fusion.5 = f32[128,512]{1,0:T(8,128)S(1)} fusion(bf16[4096,512]{1,0:T(8,128)(2,1)} %param.8, bf16[1,128,4096]{2,1,0:T(8,128)(2,1)S(1)} %copy-done), kind=kOutput, calls=%fused_computation.7 | convolution fusion | flops 536870912 | bytes 5505024 | tf_op jit(solution)/shard_map/dot_general | solution.py:59
  6.1 13.0 %all-reduce.1 = bf16[128,512]{1,0:T(8,128)(2,1)S(1)} all-reduce(f32[128,512]{1,0:T(8,128)S(1)} %fusion.5), channel_id=1, replica_groups=mesh['group'=2,'ctx'=4,'head'=2,'req'=2] {'head'}, use_global_device_ids=true, to_apply=%region_0.0 | all-reduce | flops 65536 | bytes 393216 | tf_op jit(solution)/shard_map/psum | solution.py:60
  19.1 5.8 %all_gather.9 = bf16[1,256,512]{2,1,0:T(8,128)(2,1)S(1)} all-gather(bf16[1,256,256]{2,1,0:T(8,128)(2,1)} %param.9), channel_id=1, replica_groups=mesh['group'=2,'ctx'=4,'head'=2,'req'=2] {'head'}, dimensions={2}, use_global_device_ids=true | all-gather | bytes 393216 | tf_op jit(solution)/shard_map/all_gather | solution.py:61
  24.9 0.0 copy-done.2
  24.9 0.2 convolution_convert_fusion
  25.2 0.0 copy-done.3
  25.2 0.2 fusion.18
  25.4 0.4 fusion.26
  25.9 15.7 %all_gather.10 = bf16[1536,128]{0,1:T(8,128)(2,1)S(1)} all-gather(bf16[384,128]{0,1:T(8,128)(2,1)S(1)} %pad_maximum_fusion.2), channel_id=1, replica_groups=mesh['group'=2,'ctx'=4,'head'=2,'req'=2] {'ctx'}, dimensions={0}, use_global_device_ids=true | all-gather | bytes 491520 | tf_op jit(solution)/shard_map/all_gather | solution.py:100
  41.5 15.0 %all_gather.11 = bf16[1536,128]{1,0:T(8,128)(2,1)S(1)} all-gather(bf16[384,128]{1,0:T(8,128)(2,1)S(1)} %convolution_convert_fusion), channel_id=1, replica_groups=mesh['group'=2,'ctx'=4,'head'=2,'req'=2] {'ctx'}, dimensions={0}, use_global_device_ids=true | all-gather | bytes 491520 | tf_op jit(solution)/shard_map/all_gather | solution.py:101
  56.5 0.0 copy-done.1
  56.6 0.1 copy.11
  56.7 0.3 copy.9
  57.0 0.1 subtract_convert_fusion
  57.1 1.3 %fusion = (f32[1024]{0:T(1024)S(1)}, f32[1024,1536]{1,0:T(8,128)S(1)}) fusion(s32[1536]{0:T(1024)S(1)} %le.17, s32[1024]{0:T(1024)S(1)} %broadcast_bitcast_fusion, bf16[1536,128]{0,1:T(8,128)(2,1)S(1)} %all_gather.10, bf16[1024,64]{0,1:T(8,128)(2,1)S(1)} %get-tuple-element.15, bf16[1024,64]{0,1:T(8,128)(2,1)S(1)} %get-tuple-element.16), kind=kOutput, calls=%fused_computation.2 | convolution fusion | flops 409467904 | bytes 6961152 | tf_op jit(solution)/shard_map/dot_general | solution.py:40
  58.4 2.3 %fusion.1 = f32[1024]{0:T(1024)S(1)} fusion(f32[1024,1536]{1,0:T(8,128)S(1)} %get-tuple-element.14, f32[1024]{0:T(1024)S(1)} %broadcast_maximum_fusion, s32[1536]{0:T(1024)S(1)} %le.17, s32[1024]{0:T(1024)S(1)} %broadcast_bitcast_fusion), kind=kLoop, calls=%fused_computation.3 | loop fusion | flops 9436160 | bytes 6309888 | tf_op jit(solution)/shard_map/reduce_sum | solution.py:49
  60.7 2.1 %fusion.10 = bf16[1024,128]{1,0:T(8,128)(2,1)S(1)} fusion(bf16[1536,128]{1,0:T(8,128)(2,1)S(1)} %all_gather.11, f32[1024,1536]{1,0:T(8,128)S(1)} %get-tuple-element.14, f32[1024]{0:T(1024)S(1)} %broadcast_maximum_fusion, s32[1536]{0:T(1024)S(1)} %le.17, s32[1024]{0:T(1024)S(1)} %broadcast_bitcast_fusion, f32[1024]{0:T(1024)S(1)} %fusion.1), kind=kOutput, calls=%fused_computation.10 | convolution fusion | flops 412352512 | bytes 6965248 | tf_op jit(solution)/shard_map/dot_general | solution.py:50
  62.9 0.2 copy.10
  63.0 0.8 %reshape.120 = bf16[1,128,1024]{2,1,0:T(8,128)(2,1)} reshape(bf16[128,8,128]{2,1,0:T(8,128)(2,1)S(1)} %copy.10) | data formatting | bytes 524288 | tf_op jit(solution)/shard_map/reshape | solution.py:110
  (10 shorter events, 0.1 us)
Async XLA Ops:
  0.0 3.2 %copy-start = (bf16[1,128,4096]{2,1,0:T(8,128)(2,1)S(1)}, bf16[1,128,4096]{2,1,0:T(8,128)(2,1)}, u32[]{:S(2)}) copy-start(bf16[1,128,4096]{2,1,0:T(8,128)(2,1)} %param.7) | copy-start | bytes 3145732
  0.0 56.5 %copy-start.1 = (bf16[1,128,1024]{2,1,0:T(8,128)(2,1)S(1)}, bf16[1,128,1024]{2,1,0:T(8,128)(2,1)}, u32[]{:S(2)}) copy-start(bf16[1,128,1024]{2,1,0:T(8,128)(2,1)} %param.12) | copy-start | bytes 786436
  0.0 24.9 %copy-start.2 = (bf16[1,256,128]{2,1,0:T(8,128)(2,1)S(1)}, bf16[1,256,128]{2,1,0:T(8,128)(2,1)}, u32[]{:S(2)}) copy-start(bf16[1,256,128]{2,1,0:T(8,128)(2,1)} %param.11) | copy-start | bytes 196612
  0.0 25.2 %copy-start.3 = (bf16[1,256,128]{2,1,0:T(8,128)(2,1)S(1)}, bf16[1,256,128]{2,1,0:T(8,128)(2,1)}, u32[]{:S(2)}) copy-start(bf16[1,256,128]{2,1,0:T(8,128)(2,1)} %param.10) | copy-start | bytes 196612
where the time goes:
time: 64.1 us; the launch traced here: 63.9 us
  blocking collectives  49.5 us (77%)
  matrix products  6.79 us (11%)
  other arithmetic  5.33 us (8%)
  local copies, waits for them, and re-layouts  1.42 us (2%)
  between operations  0.81 us (1%)
    all_gather x1, blocking collectives, per_device(): lax.all_gather(own_keys, 'ctx', axis=0, tiled=True)  15.7 us
    all_gather x1, blocking collectives, per_device(): lax.all_gather(own_values, 'ctx', axis=0, tiled=True)  15 us
    psum x1, blocking collectives, per_device(): fresh_lat = lax.psum(partial_value, 'head').astype(jnp.bfloat16)  13 us
    all_gather x1, blocking collectives, per_device(): cache_full = lax.all_gather(cache_latents, 'head', axis=2, tiled=True)[0]  5.85 us
    dot_general x1, matrix products, per_device(): jnp.dot(fresh_hidden[0], latent_down, preferred_element_type=jnp.float32)  2.9 us
    reduce_sum x1, other arithmetic, attend(): row_sum = jnp.sum(weights, axis=1)  2.29 us
    dot_general x1, matrix products, attend(): jnp.dot(weights.astype(jnp.bfloat16), value_rows, preferred_element_type=...  2.12 us
    mul x1, other arithmetic, per_device(): own_place * fresh_dev  1.35 us

commit v1 on v0

--- a/solution.py
+++ b/solution.py
@@ -5,6 +5,12 @@
 
 ROPE_BASE = 500000.0
 SCORE_FLOOR = -1e30
+
+
+def gather_and_add(x, axis):
+    pieces = lax.all_gather(x, axis, axis=0, tiled=False)
+    acc = pieces.sum(axis=0)
+    return acc
 
 
 def rotate(field, positions):
@@ -57,7 +63,7 @@
 
 def per_device(fresh_hidden, latent_down, cache_latents, key_up, value_up, queries, span_start):
     partial_value = jnp.dot(fresh_hidden[0], latent_down, preferred_element_type=jnp.float32)
-    fresh_lat = lax.psum(partial_value, "head").astype(jnp.bfloat16)
+    fresh_lat = gather_and_add(partial_value, "head").astype(jnp.bfloat16)
     cache_full = lax.all_gather(cache_latents, "head", axis=2, tiled=True)[0]
     local_lat = jnp.concatenate([cache_full, fresh_lat], axis=0)
     tok_dev = local_lat.shape[0]

time: 64.1 us -> 60.8 us (0.949)
  blocking collectives: 49.5 us -> 46.1 us
    psum x1 -> x0, blocking collectives: 13 us -> none  [per_device(): fresh_lat = lax.psum(partial_value, 'head').astype(jnp.bfloat16)]
    all_gather x0 -> x1, blocking collectives: none -> 9.94 us  [gather_and_add(): pieces = lax.all_gather(x, axis, axis=0, tiled=False)]
where the time goes in v1:
time: 60.8 us; the launch traced here: 60.6 us
  blocking collectives  46.1 us (76%)
  matrix products  6.78 us (11%)
  other arithmetic  5.4 us (9%)
  local copies, waits for them, and re-layouts  1.42 us (2%)
  between operations  0.83 us (1%)
    all_gather x1, blocking collectives, per_device(): lax.all_gather(own_keys, 'ctx', axis=0, tiled=True)  15.5 us
    all_gather x1, blocking collectives, per_device(): lax.all_gather(own_values, 'ctx', axis=0, tiled=True)  15.1 us
    all_gather x1, blocking collectives, gather_and_add(): pieces = lax.all_gather(x, axis, axis=0, tiled=False)  9.94 us
    all_gather x1, blocking collectives, per_device(): cache_full = lax.all_gather(cache_latents, 'head', axis=2, tiled=True)[0]  5.64 us
    dot_general x1, matrix products, per_device(): jnp.dot(fresh_hidden[0], latent_down, preferred_element_type=jnp.float32)  2.9 us
    reduce_sum x1, other arithmetic, attend(): row_sum = jnp.sum(weights, axis=1)  2.29 us
    dot_general x1, matrix products, attend(): jnp.dot(weights.astype(jnp.bfloat16), value_rows, preferred_element_type=...  2.12 us
    mul x1, other arithmetic, per_device(): own_place * fresh_dev  1.39 us

profile of v1, /device:TPU:0, one launch (start us, length us, event | category | flops | bytes accessed | tf_op | source)
XLA Modules:
  0.0 60.6 jit_solution(12137452192393633494)
XLA Ops:
  0.0 0.0 copy-start
  0.0 0.0 copy-start.1
  0.0 0.0 copy-start.3
  0.0 0.0 copy-start.4
  0.0 0.0 copy-start.2
  0.0 1.4 %fusion.38 = s32[1,1]{1,0:T(1,128)} fusion(s32[1,4]{1,0:T(1,128)} %param.13, s32[]{:T(128)S(6)} %select_n.14), kind=kLoop, calls=%fused_computation.59 | loop fusion | flops 1 | bytes 12 | tf_op jit(solution)/shard_map/mul | solution.py:81
  2.1 0.7 %multiply_bitcast_fusion = (s32[4]{0:T(128)S(1)}, s32[4]{0:T(128)S(1)}) fusion(s32[1,4]{1,0:T(1,128)} %param.13), kind=kLoop, calls=%fused_computation.50 | loop fusion | flops 12 | bytes 48 | tf_op jit(solution)/shard_map/mul | solution.py:82
  2.8 0.1 iota_add_fusion.1
  2.9 0.1 iota_add_fusion
  2.9 0.1 dynamic-slice_convert_fusion
  3.0 0.2 multiply_cosine_fusion.1
  3.2 0.0 copy-done
  3.2 2.9 %fusion.5 = f32[128,512]{1,0:T(8,128)S(1)} fusion(bf16[4096,512]{1,0:T(8,128)(2,1)} %param.8, bf16[1,128,4096]{2,1,0:T(8,128)(2,1)S(1)} %copy-done), kind=kOutput, calls=%fused_computation.7 | convolution fusion | flops 536870912 | bytes 5505024 | tf_op jit(solution)/shard_map/dot_general | solution.py:65
  6.1 9.9 %all-gather = f32[256,512]{1,0:T(8,128)S(1)} all-gather(f32[128,512]{1,0:T(8,128)S(1)} %fusion.5), channel_id=2, replica_groups=mesh['group'=2,'ctx'=4,'head'=2,'req'=2] {'head'}, dimensions={0}, use_global_device_ids=true | all-gather | bytes 786432 | tf_op jit(solution)/shard_map/all_gather | solution.py:11
  16.1 0.0 copy-done.2
  16.1 5.6 %all_gather.15 = bf16[1,256,512]{2,1,0:T(8,128)(2,1)S(1)} all-gather(bf16[1,256,256]{2,1,0:T(8,128)(2,1)S(1)} %copy-done.2), channel_id=1, replica_groups=mesh['group'=2,'ctx'=4,'head'=2,'req'=2] {'head'}, dimensions={2}, use_global_device_ids=true | all-gather | bytes 393216 | tf_op jit(solution)/shard_map/all_gather | solution.py:67
  21.8 0.0 copy-done.3
  21.8 0.2 convolution_convert_fusion
  22.0 0.0 copy-done.4
  22.0 0.2 fusion.18
  22.2 0.4 fusion.26
  22.7 15.5 %all_gather.18 = bf16[1536,128]{0,1:T(8,128)(2,1)S(1)} all-gather(bf16[384,128]{0,1:T(8,128)(2,1)S(1)} %pad_maximum_fusion.2), channel_id=1, replica_groups=mesh['group'=2,'ctx'=4,'head'=2,'req'=2] {'ctx'}, dimensions={0}, use_global_device_ids=true | all-gather | bytes 491520 | tf_op jit(solution)/shard_map/all_gather | solution.py:106
  38.2 15.1 %all_gather.19 = bf16[1536,128]{1,0:T(8,128)(2,1)S(1)} all-gather(bf16[384,128]{1,0:T(8,128)(2,1)S(1)} %convolution_convert_fusion), channel_id=1, replica_groups=mesh['group'=2,'ctx'=4,'head'=2,'req'=2] {'ctx'}, dimensions={0}, use_global_device_ids=true | all-gather | bytes 491520 | tf_op jit(solution)/shard_map/all_gather | solution.py:107
  53.2 0.0 copy-done.1
  53.3 0.1 copy.11
  53.4 0.3 copy.9
  53.7 0.1 subtract_convert_fusion
  53.8 1.3 %fusion = (f32[1024]{0:T(1024)S(1)}, f32[1024,1536]{1,0:T(8,128)S(1)}) fusion(s32[1536]{0:T(1024)S(1)} %le.17, s32[1024]{0:T(1024)S(1)} %broadcast_bitcast_fusion, bf16[1536,128]{0,1:T(8,128)(2,1)S(1)} %all_gather.18, bf16[1024,64]{0,1:T(8,128)(2,1)S(1)} %get-tuple-element.15, bf16[1024,64]{0,1:T(8,128)(2,1)S(1)} %get-tuple-element.16), kind=kOutput, calls=%fused_computation.2 | convolution fusion | flops 409467904 | bytes 6961152 | tf_op jit(solution)/shard_map/dot_general | solution.py:46
  55.1 2.3 %fusion.1 = f32[1024]{0:T(1024)S(1)} fusion(f32[1024,1536]{1,0:T(8,128)S(1)} %get-tuple-element.14, f32[1024]{0:T(1024)S(1)} %broadcast_maximum_fusion, s32[1536]{0:T(1024)S(1)} %le.17, s32[1024]{0:T(1024)S(1)} %broadcast_bitcast_fusion), kind=kLoop, calls=%fused_computation.3 | loop fusion | flops 9436160 | bytes 6309888 | tf_op jit(solution)/shard_map/reduce_sum | solution.py:55
  57.4 2.1 %fusion.10 = bf16[1024,128]{1,0:T(8,128)(2,1)S(1)} fusion(bf16[1536,128]{1,0:T(8,128)(2,1)S(1)} %all_gather.19, f32[1024,1536]{1,0:T(8,128)S(1)} %get-tuple-element.14, f32[1024]{0:T(1024)S(1)} %broadcast_maximum_fusion, s32[1536]{0:T(1024)S(1)} %le.17, s32[1024]{0:T(1024)S(1)} %broadcast_bitcast_fusion, f32[1024]{0:T(1024)S(1)} %fusion.1), kind=kOutput, calls=%fused_computation.10 | convolution fusion | flops 412352512 | bytes 6965248 | tf_op jit(solution)/shard_map/dot_general | solution.py:56
  59.6 0.2 copy.10
  59.7 0.8 %reshape.120 = bf16[1,128,1024]{2,1,0:T(8,128)(2,1)} reshape(bf16[128,8,128]{2,1,0:T(8,128)(2,1)S(1)} %copy.10) | data formatting | bytes 524288 | tf_op jit(solution)/shard_map/reshape | solution.py:116
  (11 shorter events, 0.2 us)
Async XLA Ops:
  0.0 3.2 %copy-start = (bf16[1,128,4096]{2,1,0:T(8,128)(2,1)S(1)}, bf16[1,128,4096]{2,1,0:T(8,128)(2,1)}, u32[]{:S(2)}) copy-start(bf16[1,128,4096]{2,1,0:T(8,128)(2,1)} %param.7) | copy-start | bytes 3145732
  0.0 53.2 %copy-start.1 = (bf16[1,128,1024]{2,1,0:T(8,128)(2,1)S(1)}, bf16[1,128,1024]{2,1,0:T(8,128)(2,1)}, u32[]{:S(2)}) copy-start(bf16[1,128,1024]{2,1,0:T(8,128)(2,1)} %param.12) | copy-start | bytes 786436
  0.0 21.8 %copy-start.3 = (bf16[1,256,128]{2,1,0:T(8,128)(2,1)S(1)}, bf16[1,256,128]{2,1,0:T(8,128)(2,1)}, u32[]{:S(2)}) copy-start(bf16[1,256,128]{2,1,0:T(8,128)(2,1)} %param.11) | copy-start | bytes 196612
  0.0 22.0 %copy-start.4 = (bf16[1,256,128]{2,1,0:T(8,128)(2,1)S(1)}, bf16[1,256,128]{2,1,0:T(8,128)(2,1)}, u32[]{:S(2)}) copy-start(bf16[1,256,128]{2,1,0:T(8,128)(2,1)} %param.10) | copy-start | bytes 196612
  0.0 16.1 %copy-start.2 = (bf16[1,256,256]{2,1,0:T(8,128)(2,1)S(1)}, bf16[1,256,256]{2,1,0:T(8,128)(2,1)}, u32[]{:S(2)}) copy-start(bf16[1,256,256]{2,1,0:T(8,128)(2,1)} %param.9) | copy-start | bytes 393220
